TPU v7x, 8 devices: a whole 2x2x1 slice. The times are simulated.
8 devices in a mesh: data: 1 (over z), model: 2 (over y), time: 4 (over x, core).
Axes of the slice: x: 2, y: 2, z: 1, core: 2. Of those that a mesh axis runs over, the one named last changes fastest.
Arguments:
- x_init: float32 [4, 1024, 16], P('data')
- w_up: bfloat16 [16, 1152], P(None, 'model')
- w_down: bfloat16 [1152, 16], P('model')
- mod_scale: bfloat16 [8, 1152], P('time', 'model')
- mod_shift: bfloat16 [8, 1152], P('time', 'model')
- step_size: float32 [8], P('time')
Outputs:
- output: float32 [8, 4, 1024, 16], P('time', 'data')
All inputs are finite; a program needn't handle non-finite values.
Results may differ from a plain program's by a relative error of at most 0.001.
Values are sent between devices in bfloat16 or wider.
A program may use at most 1 GiB of HBM per device.

v0:
```python
import jax
import jax.numpy as jnp
from jax import lax
from jax.sharding import PartitionSpec as P

SWEEPS = 4


def local_drift(latents, w_up, w_down, scale_f, shift_f):
    pre_act = jnp.einsum('tbnc,cd->tbnd', latents.astype(jnp.bfloat16), w_up, preferred_element_type=jnp.float32)
    hidden = jax.nn.gelu(pre_act * scale_f[:, None, None, :] + shift_f[:, None, None, :], approximate=True)
    return jnp.einsum('tbnd,dc->tbnc', hidden.astype(jnp.bfloat16), w_down, preferred_element_type=jnp.float32)


def solution(mesh):
    time_devs = mesh.shape['time']

    def device_body(x_init, w_up, w_down, mod_scale, mod_shift, step_size):
        scale_f = 1.0 + mod_scale.astype(jnp.float32)
        shift_f = mod_shift.astype(jnp.float32)
        step_col = step_size[:, None, None, None]
        latents = jnp.broadcast_to(x_init[None], (mod_scale.shape[0],) + x_init.shape)
        for sweep_idx in range(SWEEPS):
            part_drift = local_drift(latents, w_up, w_down, scale_f, shift_f)
            drifts = step_col * lax.psum(part_drift, 'model')
            running = jnp.cumsum(drifts, axis=0)
            dev_total = running[-1]
            scan_acc = dev_total
            shift_len = 1
            while shift_len < time_devs:
                perm_pairs = [(source_idx, source_idx + shift_len) for source_idx in range(time_devs - shift_len)]
                scan_acc = scan_acc + lax.ppermute(scan_acc, 'time', perm_pairs)
                shift_len = shift_len * 2
            offset = scan_acc - dev_total
            latents = (x_init + offset)[None] + (running - drifts)
        return latents

    return jax.shard_map(device_body, mesh=mesh, in_specs=(P('data', None, None), P(None, 'model'), P('model', None), P('time', 'model'), P('time', 'model'), P('time')), out_specs=P('time', 'data', None, None), check_vma=False)
```

profile of v0, /device:TPU:0, one launch (start us, length us, event | category | flops | bytes accessed | tf_op | source)
XLA Modules:
  0.0 217.0 jit_solution(657208391917557274)
XLA Ops:
  6.5 0.7 convert_add_fusion
  7.2 0.7 convert_element_type.33
  7.9 1.0 convert_element_type.31
  8.9 0.0 copy-done
  8.9 9.8 %fusion.38 = f32[2,4,1024,16]{2,3,1,0:T(8,128)} fusion(f32[2,576]{1,0:T(2,128)S(1)} %convert_element_type.33, f32[2,576]{1,0:T(2,128)S(1)} %convert_add_fusion, bf16[4,1024,16]{1,2,0:T(8,128)(2,1)S(1)} %convert_element_type.31, bf16[576,16]{0,1:T(8,128)(2,1)S(1)} %copy-done, bf16[16,576]{1,0:T(8,128)(2,1)} %param.7), kind=kOutput, calls=%fused_computation.39 | convolution fusion | flops 353894400 | bytes 701440 | tf_op jit(solution)/shard_map/tbnd,dc->tbnc/dot_general | solution.py:12
  18.7 0.0 all-reduce.5.cloned.1.call-update
  18.7 0.0 all-reduce.7.cloned.1.call-start
  18.7 25.8 %all-reduce.5.cloned.1.call-done = f32[2,4,1024,16]{2,3,1,0:T(8,128)} async-done(((f32[2,4,1024,16]{2,3,1,0:T(8,128)}), f32[2,4,1024,16]{2,3,1,0:T(8,128)}) %all-reduce.5.cloned.1.call-update) | async-done | bytes 524304 | tf_op jit(solution)/shard_map/psum | solution.py:25
  44.5 1.1 fusion.54
  45.7 0.0 copy-start.1
  45.7 1.6 collective-permute-start
  47.3 1.1 collective-permute-done
  48.5 0.0 copy-start.7
  48.5 8.7 %collective-permute-start.1 = (f32[4,1024,16]{1,2,0:T(8,128)S(1)}, f32[4,1024,16]{1,2,0:T(8,128)S(1)}, u32[]{:S(2)}, u32[]{:S(2)}) collective-permute-start(f32[4,1024,16]{1,2,0:T(8,128)S(1)} %fusion.102), channel_id=1, source_target_pairs={{0,2},{1,3},{4,6},{5,7}} | collective-permute-start | bytes 786440 | tf_op jit(solution)/shard_map/ppermute | solution.py:32
  57.3 3.7 %collective-permute-done.1 = f32[4,1024,16]{1,2,0:T(8,128)S(1)} collective-permute-done((f32[4,1024,16]{1,2,0:T(8,128)S(1)}, f32[4,1024,16]{1,2,0:T(8,128)S(1)}, u32[]{:S(2)}, u32[]{:S(2)}) %collective-permute-start.1) | collective-permute-done | bytes 262176 | tf_op jit(solution)/shard_map/ppermute | solution.py:32
  61.0 0.0 copy-done.1
  61.0 0.1 subtract_add_fusion.4
  61.0 0.0 copy-done.4
  61.0 9.1 %fusion.36 = f32[2,4,1024,16]{2,3,1,0:T(8,128)} fusion(f32[2,576]{1,0:T(2,128)S(1)} %convert_element_type.33, f32[2,576]{1,0:T(2,128)S(1)} %convert_add_fusion, f32[2,4,1024,16]{2,3,1,0:T(8,128)S(1)} %fusion.54, f32[2,4,1024,16]{2,3,1,0:T(8,128)S(1)} %copy-done.4, f32[4,1024,16]{1,2,0:T(8,128)S(1)} %subtract_add_fusion.4, f32[2]{0:T(128)S(1)} %copy-done.6, ...), kind=kOutput, calls=%fused_computation.38 | convolution fusion | flops 354418688 | bytes 1881096 | tf_op jit(solution)/shard_map/tbnd,dc->tbnc/dot_general | solution.py:12
  70.1 0.0 all-reduce.7.cloned.1.call-update
  70.1 0.0 all-reduce.9.cloned.1.call-start
  70.2 24.0 %all-reduce.7.cloned.1.call-done = f32[2,4,1024,16]{2,3,1,0:T(8,128)} async-done(((f32[2,4,1024,16]{2,3,1,0:T(8,128)}), f32[2,4,1024,16]{2,3,1,0:T(8,128)}) %all-reduce.7.cloned.1.call-update) | async-done | bytes 524304 | tf_op jit(solution)/shard_map/psum | solution.py:25
  94.2 1.1 fusion.52
  95.3 1.5 collective-permute-start.2
  96.9 1.1 collective-permute-done.2
  98.0 8.8 %collective-permute-start.3 = (f32[4,1024,16]{1,2,0:T(8,128)S(1)}, f32[4,1024,16]{1,2,0:T(8,128)S(1)}, u32[]{:S(2)}, u32[]{:S(2)}) collective-permute-start(f32[4,1024,16]{1,2,0:T(8,128)S(1)} %fusion.103), channel_id=1, source_target_pairs={{0,2},{1,3},{4,6},{5,7}} | collective-permute-start | bytes 786440 | tf_op jit(solution)/shard_map/ppermute | solution.py:32
  106.8 3.6 %collective-permute-done.3 = f32[4,1024,16]{1,2,0:T(8,128)S(1)} collective-permute-done((f32[4,1024,16]{1,2,0:T(8,128)S(1)}, f32[4,1024,16]{1,2,0:T(8,128)S(1)}, u32[]{:S(2)}, u32[]{:S(2)}) %collective-permute-start.3) | collective-permute-done | bytes 262176 | tf_op jit(solution)/shard_map/ppermute | solution.py:32
  110.4 0.1 subtract_add_fusion.3
  110.5 9.1 %fusion.34 = f32[2,4,1024,16]{2,3,1,0:T(8,128)} fusion(f32[2,576]{1,0:T(2,128)S(1)} %convert_element_type.33, f32[2,576]{1,0:T(2,128)S(1)} %convert_add_fusion, f32[2,4,1024,16]{2,3,1,0:T(8,128)S(1)} %fusion.52, f32[2,4,1024,16]{2,3,1,0:T(8,128)S(1)} %copy-done.5, f32[4,1024,16]{1,2,0:T(8,128)S(1)} %subtract_add_fusion.3, f32[2]{0:T(128)S(1)} %copy-done.6, ...), kind=kOutput, calls=%fused_computation.37 | convolution fusion | flops 354418688 | bytes 1881096 | tf_op jit(solution)/shard_map/tbnd,dc->tbnc/dot_general | solution.py:12
  119.6 0.0 all-reduce.9.cloned.1.call-update
  119.6 0.0 all-reduce.11.cloned.1.call-start
  119.7 24.0 %all-reduce.9.cloned.1.call-done = f32[2,4,1024,16]{2,3,1,0:T(8,128)} async-done(((f32[2,4,1024,16]{2,3,1,0:T(8,128)}), f32[2,4,1024,16]{2,3,1,0:T(8,128)}) %all-reduce.9.cloned.1.call-update) | async-done | bytes 524304 | tf_op jit(solution)/shard_map/psum | solution.py:25
  143.6 1.1 fusion.50
  144.8 1.5 collective-permute-start.4
  146.3 1.1 collective-permute-done.4
  147.5 8.8 %collective-permute-start.5 = (f32[4,1024,16]{1,2,0:T(8,128)S(1)}, f32[4,1024,16]{1,2,0:T(8,128)S(1)}, u32[]{:S(2)}, u32[]{:S(2)}) collective-permute-start(f32[4,1024,16]{1,2,0:T(8,128)S(1)} %fusion.104), channel_id=1, source_target_pairs={{0,2},{1,3},{4,6},{5,7}} | collective-permute-start | bytes 786440 | tf_op jit(solution)/shard_map/ppermute | solution.py:32
  156.4 3.6 %collective-permute-done.5 = f32[4,1024,16]{1,2,0:T(8,128)S(1)} collective-permute-done((f32[4,1024,16]{1,2,0:T(8,128)S(1)}, f32[4,1024,16]{1,2,0:T(8,128)S(1)}, u32[]{:S(2)}, u32[]{:S(2)}) %collective-permute-start.5) | collective-permute-done | bytes 262176 | tf_op jit(solution)/shard_map/ppermute | solution.py:32
  159.9 0.1 subtract_add_fusion.2
  160.0 9.1 %fusion.32 = f32[2,4,1024,16]{2,3,1,0:T(8,128)} fusion(f32[2,576]{1,0:T(2,128)S(1)} %convert_element_type.33, f32[2,576]{1,0:T(2,128)S(1)} %convert_add_fusion, f32[2,4,1024,16]{2,3,1,0:T(8,128)S(1)} %fusion.50, f32[2,4,1024,16]{2,3,1,0:T(8,128)S(1)} %copy-done.3, f32[4,1024,16]{1,2,0:T(8,128)S(1)} %subtract_add_fusion.2, f32[2]{0:T(128)S(1)} %copy-done.6, ...), kind=kOutput, calls=%fused_computation.36 | convolution fusion | flops 354418688 | bytes 1881096 | tf_op jit(solution)/shard_map/tbnd,dc->tbnc/dot_general | solution.py:12
  169.1 0.0 all-reduce.11.cloned.1.call-update
  169.1 24.0 %all-reduce.11.cloned.1.call-done = f32[2,4,1024,16]{2,3,1,0:T(8,128)} async-done(((f32[2,4,1024,16]{2,3,1,0:T(8,128)}), f32[2,4,1024,16]{2,3,1,0:T(8,128)}) %all-reduce.11.cloned.1.call-update) | async-done | bytes 524304 | tf_op jit(solution)/shard_map/psum | solution.py:25
  193.1 1.1 fusion.48
  194.3 1.5 collective-permute-start.6
  195.8 1.1 collective-permute-done.6
  197.0 8.6 %collective-permute-start.7 = (f32[4,1024,16]{1,2,0:T(8,128)S(1)}, f32[4,1024,16]{1,2,0:T(8,128)S(1)}, u32[]{:S(2)}, u32[]{:S(2)}) collective-permute-start(f32[4,1024,16]{1,2,0:T(8,128)S(1)} %fusion.105), channel_id=1, source_target_pairs={{0,2},{1,3},{4,6},{5,7}} | collective-permute-start | bytes 786440 | tf_op jit(solution)/shard_map/ppermute | solution.py:32
  205.6 3.8 %collective-permute-done.7 = f32[4,1024,16]{1,2,0:T(8,128)S(1)} collective-permute-done((f32[4,1024,16]{1,2,0:T(8,128)S(1)}, f32[4,1024,16]{1,2,0:T(8,128)S(1)}, u32[]{:S(2)}, u32[]{:S(2)}) %collective-permute-start.7) | collective-permute-done | bytes 262176 | tf_op jit(solution)/shard_map/ppermute | solution.py:32
  209.4 0.1 subtract_add_fusion.1
  209.5 1.0 subtract_add_fusion
  (20 shorter events, 0.3 us)
Async XLA Ops:
  6.5 2.4 %copy-start = (bf16[576,16]{0,1:T(8,128)(2,1)S(1)}, bf16[576,16]{0,1:T(8,128)(2,1)}, u32[]{:S(2)}) copy-start(bf16[576,16]{0,1:T(8,128)(2,1)} %param.8) | copy-start | bytes 55300
  6.5 38.0 %all-reduce.5.cloned.1.call-start = ((), (), s32[]{:S(2)}) async-start(), calls=%async_computation | async-start | bytes 1048576 | tf_op jit(solution)/shard_map/psum | solution.py:25
  18.7 25.9 %copy-start.6 = (f32[2]{0:T(128)S(1)}, f32[2]{0:T(128)}, u32[]{:S(2)}) copy-start(f32[2]{0:T(128)} %param.11) | copy-start | bytes 28
  18.7 75.5 %all-reduce.7.cloned.1.call-start = ((), (), s32[]{:S(2)}) async-start(), calls=%async_computation.1 | async-start | bytes 1048576 | tf_op jit(solution)/shard_map/psum | solution.py:25
  45.7 15.3 %copy-start.1 = (f32[4,1024,16]{1,2,0:T(8,128)S(1)}, f32[4,1024,16]{1,2,0:T(8,128)}, u32[]{:S(2)}) copy-start(f32[4,1024,16]{1,2,0:T(8,128)} %param.6) | copy-start | bytes 786436
  45.7 2.8 %collective-permute-start = (f32[4,1024,16]{1,2,0:T(8,128)S(1)}, f32[4,1024,16]{1,2,0:T(8,128)S(1)}, u32[]{:S(2)}, u32[]{:S(2)}) collective-permute-start(f32[4,1024,16]{1,2,0:T(8,128)S(1)} %slice_bitcast_fusion.3), channel_id=1, source_target_pairs={{0,1},{1,2},{2,3},{4,5},{5,6},{6,7}} | collective-permute-start | bytes 786440 | tf_op jit(solution)/shard_map/ppermute | solution.py:32
  48.5 12.5 %copy-start.4 = (f32[2,4,1024,16]{2,3,1,0:T(8,128)S(1)}, f32[2,4,1024,16]{2,3,1,0:T(8,128)}, u32[]{:S(2)}) copy-start(f32[2,4,1024,16]{2,3,1,0:T(8,128)} %all-reduce.5.cloned.1.call-done) | copy-start | bytes 1572868
  48.5 12.5 %copy-start.7 = (bf16[16,576]{1,0:T(8,128)(2,1)S(1)}, bf16[16,576]{1,0:T(8,128)(2,1)}, u32[]{:S(2)}) copy-start(bf16[16,576]{1,0:T(8,128)(2,1)} %param.7) | copy-start | bytes 55300
  48.5 12.4 %collective-permute-start.1 = (f32[4,1024,16]{1,2,0:T(8,128)S(1)}, f32[4,1024,16]{1,2,0:T(8,128)S(1)}, u32[]{:S(2)}, u32[]{:S(2)}) collective-permute-start(f32[4,1024,16]{1,2,0:T(8,128)S(1)} %fusion.102), channel_id=1, source_target_pairs={{0,2},{1,3},{4,6},{5,7}} | collective-permute-start | bytes 786440 | tf_op jit(solution)/shard_map/ppermute | solution.py:32
  70.1 73.5 %all-reduce.9.cloned.1.call-start = ((), (), s32[]{:S(2)}) async-start(), calls=%async_computation.2 | async-start | bytes 1048576 | tf_op jit(solution)/shard_map/psum | solution.py:25
  95.3 2.6 %collective-permute-start.2 = (f32[4,1024,16]{1,2,0:T(8,128)S(1)}, f32[4,1024,16]{1,2,0:T(8,128)S(1)}, u32[]{:S(2)}, u32[]{:S(2)}) collective-permute-start(f32[4,1024,16]{1,2,0:T(8,128)S(1)} %slice_bitcast_fusion.2), channel_id=1, source_target_pairs={{0,1},{1,2},{2,3},{4,5},{5,6},{6,7}} | collective-permute-start | bytes 786440 | tf_op jit(solution)/shard_map/ppermute | solution.py:32
  98.0 12.5 %copy-start.5 = (f32[2,4,1024,16]{2,3,1,0:T(8,128)S(1)}, f32[2,4,1024,16]{2,3,1,0:T(8,128)}, u32[]{:S(2)}) copy-start(f32[2,4,1024,16]{2,3,1,0:T(8,128)} %all-reduce.7.cloned.1.call-done) | copy-start | bytes 1572868
  98.0 12.4 %collective-permute-start.3 = (f32[4,1024,16]{1,2,0:T(8,128)S(1)}, f32[4,1024,16]{1,2,0:T(8,128)S(1)}, u32[]{:S(2)}, u32[]{:S(2)}) collective-permute-start(f32[4,1024,16]{1,2,0:T(8,128)S(1)} %fusion.103), channel_id=1, source_target_pairs={{0,2},{1,3},{4,6},{5,7}} | collective-permute-start | bytes 786440 | tf_op jit(solution)/shard_map/ppermute | solution.py:32
  119.6 73.5 %all-reduce.11.cloned.1.call-start = ((), (), s32[]{:S(2)}) async-start(), calls=%async_computation.3 | async-start | bytes 1048576 | tf_op jit(solution)/shard_map/psum | solution.py:25
  144.8 2.6 %collective-permute-start.4 = (f32[4,1024,16]{1,2,0:T(8,128)S(1)}, f32[4,1024,16]{1,2,0:T(8,128)S(1)}, u32[]{:S(2)}, u32[]{:S(2)}) collective-permute-start(f32[4,1024,16]{1,2,0:T(8,128)S(1)} %slice_bitcast_fusion.1), channel_id=1, source_target_pairs={{0,1},{1,2},{2,3},{4,5},{5,6},{6,7}} | collective-permute-start | bytes 786440 | tf_op jit(solution)/shard_map/ppermute | solution.py:32
  147.5 12.5 %copy-start.3 = (f32[2,4,1024,16]{2,3,1,0:T(8,128)S(1)}, f32[2,4,1024,16]{2,3,1,0:T(8,128)}, u32[]{:S(2)}) copy-start(f32[2,4,1024,16]{2,3,1,0:T(8,128)} %all-reduce.9.cloned.1.call-done) | copy-start | bytes 1572868
  147.5 12.4 %collective-permute-start.5 = (f32[4,1024,16]{1,2,0:T(8,128)S(1)}, f32[4,1024,16]{1,2,0:T(8,128)S(1)}, u32[]{:S(2)}, u32[]{:S(2)}) collective-permute-start(f32[4,1024,16]{1,2,0:T(8,128)S(1)} %fusion.104), channel_id=1, source_target_pairs={{0,2},{1,3},{4,6},{5,7}} | collective-permute-start | bytes 786440 | tf_op jit(solution)/shard_map/ppermute | solution.py:32
  194.3 2.6 %collective-permute-start.6 = (f32[4,1024,16]{1,2,0:T(8,128)S(1)}, f32[4,1024,16]{1,2,0:T(8,128)S(1)}, u32[]{:S(2)}, u32[]{:S(2)}) collective-permute-start(f32[4,1024,16]{1,2,0:T(8,128)S(1)} %slice_bitcast_fusion), channel_id=1, source_target_pairs={{0,1},{1,2},{2,3},{4,5},{5,6},{6,7}} | collective-permute-start | bytes 786440 | tf_op jit(solution)/shard_map/ppermute | solution.py:32
  197.0 12.5 %copy-start.2 = (f32[2,4,1024,16]{2,3,1,0:T(8,128)S(1)}, f32[2,4,1024,16]{2,3,1,0:T(8,128)}, u32[]{:S(2)}) copy-start(f32[2,4,1024,16]{2,3,1,0:T(8,128)} %all-reduce.11.cloned.1.call-done) | copy-start | bytes 1572868
  197.0 12.4 %collective-permute-start.7 = (f32[4,1024,16]{1,2,0:T(8,128)S(1)}, f32[4,1024,16]{1,2,0:T(8,128)S(1)}, u32[]{:S(2)}, u32[]{:S(2)}) collective-permute-start(f32[4,1024,16]{1,2,0:T(8,128)S(1)} %fusion.105), channel_id=1, source_target_pairs={{0,2},{1,3},{4,6},{5,7}} | collective-permute-start | bytes 786440 | tf_op jit(solution)/shard_map/ppermute | solution.py:32
Sparse Core Ops, SparseCore 0:
  18.8 25.6 all-reduce.4
  70.3 23.8 all-reduce.6
  119.7 23.8 all-reduce.8
  169.2 23.8 all-reduce.10
where the time goes:
time: 218 us; the launch traced here: 217 us
  waiting for transfers between devices  117 us (54%)
  starting transfers between devices  41.2 us (19%)
  matrix products  37 us (17%)
  between operations  13.4 us (6%)
  other arithmetic  8.33 us (4%)
    psum x4, waiting for transfers between devices, device_body(): drifts = step_col * lax.psum(part_drift, 'model')  97.7 us
    ppermute x8, starting transfers between devices, device_body(): scan_acc = scan_acc + lax.ppermute(scan_acc, 'time', perm_pairs)  41.1 us
    dot_general x4, matrix products, local_drift(): jnp.einsum('tbnd,dc->tbnc', hidden.astype(jnp.bfloat16), w_down, preferre...  37 us
    ppermute x8, waiting for transfers between devices, device_body(): scan_acc = scan_acc + lax.ppermute(scan_acc, 'time', perm_pairs)  19.2 us
    another operation x4, other arithmetic, device_body(): running = jnp.cumsum(drifts, axis=0)  4.58 us
  transfers between devices with their start and end apart: 12, of which 12 were waited for; matrix products, arithmetic and copies ran while one was open for 0% of the time, Pallas kernels for 0%

commit v1 on v0

v1 whole, which is shorter than its diff:
```python
import functools

import jax
import jax.numpy as jnp
from jax import lax
from jax.experimental import pallas as pl
from jax.experimental.pallas import tpu as pltpu
from jax.sharding import PartitionSpec as P

MESH = pl.DeviceIdType.MESH
SWEEPS = 4
STEPS = 8
NM, NT = 2, 4
BATCH, TOKENS, CHAN = 4, 1024, 16
HALF = 576
BODY = 512
HIDDEN = 2 * HALF
DEV_TOK = BATCH * TOKENS // (NM * NT)
CHUNKS = 2
TM = DEV_TOK // CHUNKS
ROW = 640
HID_TILE = 256
TANH_LIN = 0.7978845608028654
TANH_CUB = TANH_LIN * 0.044715


def twice_gelu_half(half):
    inner = half * ((8.0 * TANH_CUB) * (half * half) + 2.0 * TANH_LIN)
    return half * jnp.tanh(inner) + half


def drift(x_rows, step, w_up, w_down_t, scale, shift):
    total = None
    for lo in range(0, HIDDEN, HID_TILE):
        cols = slice(lo, min(lo + HID_TILE, HIDDEN))
        pre = jnp.dot(x_rows, w_up[:, cols], preferred_element_type=jnp.float32)
        hidden = twice_gelu_half(pre * scale[step:step + 1, cols] + shift[step:step + 1, cols])
        part = lax.dot_general(w_down_t[:, cols], hidden.astype(jnp.bfloat16), (((1,), (1,)), ((), ())),
                               preferred_element_type=jnp.float32)
        total = part if total is None else total + part
    return total


def join_halves(a, b):
    return jnp.concatenate([a[:, :BODY], b[:, :BODY], a[:, BODY:HALF], b[:, BODY:HALF]], axis=1)


def kernel(x_ref, up_ref, down_ref, gam_ref, bet_ref, step_ref, out_ref,
           x0, up_half, down_half, row_loc, rows, w_up, w_down_t, scale, shift, final,
           loc_sem, psend, precv, wsend, wrecv, osend, orecv):
    me_m = lax.axis_index("model")
    me_t = lax.axis_index("time")
    me = me_m * NT + me_t
    sample = me // 2
    tok0 = pl.multiple_of((me % 2) * DEV_TOK, DEV_TOK)

    def peer(dm, dt):
        return (0, (me_m + dm) % NM, (me_t + dt) % NT)

    others = [(dm, dt) for dm in range(NM) for dt in range(NT) if (dm, dt) != (0, 0)]

    barrier = pltpu.get_barrier_semaphore()
    for dm, dt in others:
        pl.semaphore_signal(barrier, inc=1, device_id=peer(dm, dt), device_id_type=MESH)

    x_copy = pltpu.make_async_copy(x_ref.at[sample, :, pl.ds(tok0, DEV_TOK)], x0, loc_sem.at[0])
    x_copy.start()

    row_loc[0:2, 0:HALF] = 0.5 * (1.0 + gam_ref[...].astype(jnp.float32))
    row_loc[2:4, 0:HALF] = 0.5 * bet_ref[...].astype(jnp.float32)
    for r in range(2):
        row_loc[r:r + 1, HALF:ROW] = jnp.full((1, ROW - HALF), step_ref[r], jnp.float32)
    rows[me_m, me_t] = row_loc[...]
    up_half[me_m] = up_ref[...]
    down_half[me_m] = down_ref[...]

    pl.semaphore_wait(barrier, len(others))

    sends = []
    for n, (dm, dt) in enumerate(others):
        copy = pltpu.make_async_remote_copy(row_loc, rows.at[me_m, me_t], psend.at[n], precv.at[n],
                                            device_id=peer(dm, dt), device_id_type=MESH)
        copy.start()
        sends.append(copy)
    for n, (src, dst) in enumerate(((up_ref, up_half), (down_ref, down_half))):
        copy = pltpu.make_async_remote_copy(src, dst.at[me_m], wsend.at[n], wrecv.at[n],
                                            device_id=peer(1, 0), device_id_type=MESH)
        copy.start()
        sends.append(copy)
    for copy in sends:
        copy.wait_recv()
    x_copy.wait()

    @pl.when(me_t == 0)
    def _():
        copy = pltpu.make_async_copy(x_ref, out_ref.at[0], loc_sem.at[1])
        copy.start()
        copy.wait()

    w_up[...] = join_halves(up_half[0], up_half[1])
    w_down_t[...] = join_halves(down_half[0], down_half[1])
    for t in range(NT):
        scale[2 * t:2 * t + 2, :] = join_halves(rows[0, t, 0:2, :], rows[1, t, 0:2, :])
        shift[2 * t:2 * t + 2, :] = join_halves(rows[0, t, 2:4, :], rows[1, t, 2:4, :])

    out_copies = []

    def place(j, c):
        return out_ref.at[j % 2, sample, :, pl.ds(pl.multiple_of(tok0 + c * TM, TM), TM)]

    def publish(j, c, value):
        owner = j // 2
        src = final.at[c, j]
        src[...] = value
        dt = (owner + NT - me_t) % NT
        far = pltpu.make_async_remote_copy(src, place(j, c), osend.at[j, c, 0], orecv.at[1, dt, j % 2, c],
                                           device_id=(0, (me_m + 1) % NM, owner), device_id_type=MESH)
        far.start()
        near = pltpu.make_async_remote_copy(src, place(j, c), osend.at[j, c, 1], orecv.at[0, dt, j % 2, c],
                                            device_id=(0, me_m, owner), device_id_type=MESH)
        out_copies.append((owner, far, near))

        @pl.when(me_t != owner)
        def _():
            near.start()

        @pl.when(me_t == owner)
        def _():
            place(j, c)[...] = value

    for c in range(CHUNKS):
        start = x0[:, c * TM:(c + 1) * TM]
        latents = {j: start for j in range(SWEEPS)}
        settled = jnp.zeros_like(start)
        for sweep in range(1, SWEEPS + 1):
            running = settled
            fresh = {}
            for j in range(sweep - 1, sweep + 3):
                value = drift(latents[j].T.astype(jnp.bfloat16), j, w_up, w_down_t, scale, shift)
                running = running + rows[0, j // 2, j % 2:j % 2 + 1, HALF:HALF + 1] * value
                fresh[j + 1] = start + running
                if j == sweep - 1:
                    settled = running
                if j == sweep - 1 or sweep == SWEEPS:
                    publish(j + 1, c, fresh[j + 1])
            latents = fresh

    for copy in sends:
        copy.wait_send()
    for owner, far, near in out_copies:
        far.wait_send()

        @pl.when(me_t != owner)
        def _():
            near.wait_send()

    for r in range(2):
        def arrivals():
            for dm, dt in others:
                for c in range(CHUNKS):
                    pltpu.make_async_remote_copy(final.at[c, r], place(r, c), osend.at[0, 0, 0], orecv.at[dm, dt, r, c],
                                                 device_id=peer(dm, dt), device_id_type=MESH).wait_recv()
        if r == 0:
            pl.when(me_t > 0)(arrivals)
        else:
            arrivals()


def solution(mesh):
    def device_body(x_init, w_up, w_down, mod_scale, mod_shift, step_size):
        x_t = jnp.swapaxes(x_init, 1, 2)
        vmem = pl.BlockSpec(memory_space=pltpu.VMEM)
        out = pl.pallas_call(
            kernel,
            out_shape=jax.ShapeDtypeStruct((2, BATCH, CHAN, TOKENS), jnp.float32),
            in_specs=[pl.BlockSpec(memory_space=pl.ANY), vmem, vmem, vmem, vmem, pl.BlockSpec(memory_space=pltpu.SMEM)],
            out_specs=vmem,
            scratch_shapes=[
                pltpu.VMEM((CHAN, DEV_TOK), jnp.float32),
                pltpu.VMEM((NM, CHAN, HALF), jnp.bfloat16),
                pltpu.VMEM((NM, CHAN, HALF), jnp.bfloat16),
                pltpu.VMEM((4, ROW), jnp.float32),
                pltpu.VMEM((NM, NT, 4, ROW), jnp.float32),
                pltpu.VMEM((CHAN, HIDDEN), jnp.bfloat16),
                pltpu.VMEM((CHAN, HIDDEN), jnp.bfloat16),
                pltpu.VMEM((STEPS, HIDDEN), jnp.float32),
                pltpu.VMEM((STEPS, HIDDEN), jnp.float32),
                pltpu.VMEM((CHUNKS, STEPS, CHAN, TM), jnp.float32),
                pltpu.SemaphoreType.DMA((2,)),
                pltpu.SemaphoreType.DMA((7,)),
                pltpu.SemaphoreType.DMA((7,)),
                pltpu.SemaphoreType.DMA((2,)),
                pltpu.SemaphoreType.DMA((2,)),
                pltpu.SemaphoreType.DMA((STEPS, CHUNKS, 2)),
                pltpu.SemaphoreType.DMA((NM, NT, 2, CHUNKS)),
            ],
            compiler_params=pltpu.CompilerParams(collective_id=0, has_side_effects=True),
        )(x_t, w_up, w_down.T, mod_scale, mod_shift, step_size)
        return jnp.swapaxes(out, 2, 3)

    return jax.shard_map(device_body, mesh=mesh, in_specs=(P('data', None, None), P(None, 'model'), P('model', None), P('time', 'model'), P('time', 'model'), P('time')), out_specs=P('time', 'data', None, None), check_vma=False)
```

time: 218 us -> 38.6 us (0.18)
  the two profiles are of different devices: /device:TPU:0 before, /device:TPU:3 now
where the time goes in v1:
time: 38.6 us; the launch traced here: 38.1 us
  Pallas kernels  36.2 us (94%)
  local copies, waits for them, and re-layouts  1.89 us (5%)
    pallas_call x1, Pallas kernels, device_body(): pl.pallas_call(kernel, out_shape=jax.ShapeDtypeStruct((2, BATCH, CHAN, TO...  36.2 us
    unnamed x1, local copies, waits for them, and re-layouts  1.89 us

profile of v1, /device:TPU:3, one launch (start us, length us, event | category | flops | bytes accessed | tf_op | source)
XLA Modules:
  0.0 38.1 jit_solution(8214278021324813396)
XLA Ops:
  0.0 36.2 %shard_map.64 = f32[2,4,16,1024]{3,2,1,0:T(8,128)} custom-call(f32[4,16,1024]{2,1,0:T(8,128)} %bitcast.4, bf16[16,576]{1,0:T(8,128)(2,1)} %up_ref.1, bf16[16,576]{1,0:T(8,128)(2,1)} %bitcast.5, bf16[2,576]{1,0:T(2,128)(2,1)} %gam_ref.1, bf16[2,576]{1,0:T(2,128)(2,1)} %bet_ref.1, f32[2]{0:T(128)} %step_ref.1), custom_call_target="tpu_custom_call" | custom-call | tf_op jit(solution)/shard_map/pallas_call | solution.py:173
  36.2 1.9 %copy.8 = f32[2,4,1024,16]{2,3,1,0:T(8,128)} copy(f32[2,4,1024,16]{2,3,1,0:T(8,128)} %bitcast.3) | data formatting | bytes 1048576

commit v2 on v1

v2 whole, which is shorter than its diff:
```python
import jax
import jax.numpy as jnp
from jax import lax
from jax.experimental import pallas as pl
from jax.experimental.pallas import tpu as pltpu
from jax.sharding import PartitionSpec as P

MESH = pl.DeviceIdType.MESH
SWEEPS = 4
STEPS = 8
NM, NT = 2, 4
BATCH, TOKENS, CHAN = 4, 1024, 16
HALF = 576
BODY = 512
HIDDEN = 2 * HALF
DEV_TOK = BATCH * TOKENS // (NM * NT)
CHUNKS = 2
TM = DEV_TOK // CHUNKS
HID_TILE = 1152
TANH_LIN = 0.7978845608028654
TANH_CUB = TANH_LIN * 0.044715


def gelu_from_half(half):
    inner = half * ((8.0 * TANH_CUB) * (half * half) + 2.0 * TANH_LIN)
    return half * jnp.tanh(inner) + half


def drift(x_rows, scale_row, shift_row, w_up, w_down_t, lo, hi, tile=HID_TILE):
    total = None
    for at in range(lo, hi, tile):
        cols = slice(at, min(at + tile, hi))
        pre = jnp.dot(x_rows, w_up[:, cols], preferred_element_type=jnp.float32)
        hidden = gelu_from_half(pre * scale_row[:, cols] + shift_row[:, cols])
        part = lax.dot_general(w_down_t[:, cols], hidden.astype(jnp.bfloat16), (((1,), (1,)), ((), ())),
                               preferred_element_type=jnp.float32)
        total = part if total is None else total + part
    return total


def kernel(x_ref, up_ref, down_ref, gam_ref, bet_ref, step_ref, out_ref,
           x0, w_own, w_other, rows, steps, w_up, w_down_t, scale, shift, first, final,
           loc_sem, rsend, rrecv, hsend, hrecv, wsend, wrecv, osend, orecv):
    me_m = lax.axis_index("model")
    me_t = lax.axis_index("time")
    me = me_m * NT + me_t
    sample = me // 2
    tok0 = pl.multiple_of((me % 2) * DEV_TOK, DEV_TOK)

    def peer(dm, dt):
        return (0, (me_m + dm) % NM, (me_t + dt) % NT)

    others = [(dm, dt) for dm in range(NM) for dt in range(NT) if (dm, dt) != (0, 0)]

    barrier = pltpu.get_barrier_semaphore()
    for dm, dt in others:
        pl.semaphore_signal(barrier, inc=1, device_id=peer(dm, dt), device_id_type=MESH)

    local = [pltpu.make_async_copy(src, dst, loc_sem.at[n]) for n, (src, dst) in enumerate((
        (gam_ref, rows.at[0, me_t, 0]), (bet_ref, rows.at[0, me_t, 1]), (up_ref, w_own.at[0]), (down_ref, w_own.at[1]),
        (x_ref.at[sample, :, pl.ds(tok0, DEV_TOK)], x0), (step_ref, steps.at[me_t])))]
    for copy in local:
        copy.start()
    keep = pltpu.make_async_copy(x_ref, out_ref.at[0], loc_sem.at[6])

    @pl.when(me_t == 0)
    def _():
        keep.start()

    for copy in local:
        copy.wait()

    def table(half, t, cols, src):
        scale[t, :, cols] = 0.5 * (1.0 + rows[half, t, 0].astype(jnp.float32)[:, src])
        shift[t, :, cols] = 0.5 * rows[half, t, 1].astype(jnp.float32)[:, src]

    own_cols = slice(0, BODY)

    def first_pair(t):
        table(0, t, own_cols, own_cols)
        for r in range(2):
            for c in range(CHUNKS):
                tok = slice(c * TM, (c + 1) * TM)
                first[t, r, :, tok] = drift(x0[:, tok].T.astype(jnp.bfloat16), scale[t, r:r + 1, :], shift[t, r:r + 1, :],
                                            w_up, w_down_t, 0, BODY)

    w_up[:, own_cols] = w_own[0][:, own_cols]
    w_down_t[:, own_cols] = w_own[1][:, own_cols]

    @pl.when(me_t < 2)
    def _():
        first_pair(me_t)

    pl.semaphore_wait(barrier, len(others))

    sends = []

    def send(src, dst, ssem, rsem, to):
        copy = pltpu.make_async_remote_copy(src, dst, ssem, rsem, device_id=to, device_id_type=MESH)
        copy.start()
        sends.append(copy)

    def arrived(buf, sem):
        pltpu.make_async_remote_copy(buf, buf, rsend.at[0, 0], sem, device_id=peer(1, 0), device_id_type=MESH).wait_recv()

    mine = rows.at[0, me_t]
    for dt in (2, 3, 1):
        send(mine, mine, rsend.at[0, dt], rrecv.at[0, me_t], peer(0, dt))
    for dt in (2, 3, 1, 0):
        send(mine, rows.at[1, me_t], rsend.at[1, dt], rrecv.at[1, me_t], peer(1, dt))
    send(w_own, w_other, wsend, wrecv, peer(1, 0))
    for dt in (2, 3, 1):
        send(steps.at[me_t], steps.at[me_t], hsend.at[dt], hrecv.at[me_t], peer(0, dt))

    def rows_arrived(half, t):
        if half == 1:
            arrived(rows.at[1, t], rrecv.at[1, t])
        else:
            @pl.when(me_t != t)
            def _():
                arrived(rows.at[0, t], rrecv.at[0, t])

    rows_arrived(0, 0)
    rows_arrived(0, 1)
    first_pair(jnp.where(me_t < 2, 1 - me_t, 0))

    @pl.when(me_t >= 2)
    def _():
        first_pair(1)

    arrived(w_other, wrecv)
    rows_arrived(1, 0)
    rows_arrived(1, 1)

    other_cols = slice(BODY, 2 * BODY)
    rest = slice(BODY, HALF)
    rest_cols = slice(2 * BODY, HIDDEN)

    def join(a, b):
        return jnp.concatenate([a[:, rest], b[:, rest]], axis=1)

    for n, dst in enumerate((w_up, w_down_t)):
        dst[:, other_cols] = w_other[n][:, own_cols]
        dst[:, rest_cols] = join(w_own[n], w_other[n])

    def finish_table(t):
        table(1, t, other_cols, own_cols)
        scale[t, :, rest_cols] = 0.5 * (1.0 + join(rows[0, t, 0].astype(jnp.float32), rows[1, t, 0].astype(jnp.float32)))
        shift[t, :, rest_cols] = 0.5 * join(rows[0, t, 1].astype(jnp.float32), rows[1, t, 1].astype(jnp.float32))

    for t in range(2):
        finish_table(t)

    def evaluate(latent, j, lo):
        return drift(latent.T.astype(jnp.bfloat16), scale[j // 2, j % 2:j % 2 + 1, :], shift[j // 2, j % 2:j % 2 + 1, :],
                     w_up, w_down_t, lo, HIDDEN)

    def step_value(j):
        return steps[j // 2, :, j % 2:j % 2 + 1]

    out_copies = []

    def place(j, c):
        return out_ref.at[j % 2, sample, :, pl.ds(pl.multiple_of(tok0 + c * TM, TM), TM)]

    def publish(j, c, value):
        owner = j // 2
        src = final.at[c, j]
        src[...] = value
        dt = (owner + NT - me_t) % NT
        far = pltpu.make_async_remote_copy(src, place(j, c), osend.at[j, c, 0], orecv.at[1, dt, j % 2, c],
                                           device_id=(0, (me_m + 1) % NM, owner), device_id_type=MESH)
        far.start()
        near = pltpu.make_async_remote_copy(src, place(j, c), osend.at[j, c, 1], orecv.at[0, dt, j % 2, c],
                                            device_id=(0, me_m, owner), device_id_type=MESH)
        out_copies.append((owner, far, near))

        @pl.when(me_t != owner)
        def _():
            near.start()

    starts = [x0[:, c * TM:(c + 1) * TM] for c in range(CHUNKS)]
    settled = [None] * CHUNKS
    running = [None] * CHUNKS

    def sweep_step(sweep, j, c, value):
        value = step_value(j) * value
        if j == sweep - 1:
            running[c] = settled[c]
        running[c] = value if running[c] is None else running[c] + value
        fresh[c][j + 1] = starts[c] + running[c]
        if j == sweep - 1:
            settled[c] = running[c]
        if j == sweep - 1 or sweep == SWEEPS:
            publish(j + 1, c, fresh[c][j + 1])

    for t in range(2):
        @pl.when(me_t != t)
        def _():
            arrived(steps.at[t], hrecv.at[t])
    fresh = [{} for _ in range(CHUNKS)]
    for j in range(SWEEPS):
        for c in range(CHUNKS):
            value = first[j // 2, j % 2, :, c * TM:(c + 1) * TM] + evaluate(starts[c], j, BODY)
            sweep_step(1, j, c, value)

    for t in range(2, NT):
        rows_arrived(0, t)
        rows_arrived(1, t)

        @pl.when(me_t != t)
        def _():
            arrived(steps.at[t], hrecv.at[t])

        table(0, t, own_cols, own_cols)
        finish_table(t)

    latents = [None] * CHUNKS
    for c, n in ORDER:
        sweep, j = n // 4 + 1, n // 4 + n % 4
        if n % 4 == 0:
            latents[c] = fresh[c]
            fresh[c] = {}
        sweep_step(sweep, j, c, evaluate(latents[c][j], j, 0))

    for j in range(1, STEPS):
        @pl.when(me_t == j // 2)
        def _():
            for c in range(CHUNKS):
                place(j, c)[...] = final[c, j]

    for copy in sends:
        copy.wait_send()
    for owner, far, near in out_copies:
        far.wait_send()

        @pl.when(me_t != owner)
        def _():
            near.wait_send()

    @pl.when(me_t == 0)
    def _():
        keep.wait()

    for r in range(2):
        def arrivals():
            for dm, dt in others:
                for c in range(CHUNKS):
                    arrived(place(r, c), orecv.at[dm, dt, r, c])
        if r == 0:
            pl.when(me_t > 0)(arrivals)
        else:
            arrivals()


ORDER = [(c, n) for c in range(CHUNKS) for n in range(4, 16)]


def solution(mesh):
    def device_body(x_init, w_up, w_down, mod_scale, mod_shift, step_size):
        x_t = jnp.swapaxes(x_init, 1, 2)
        anywhere = pl.BlockSpec(memory_space=pl.ANY)
        out = pl.pallas_call(
            kernel,
            out_shape=pltpu.VMEM((2, BATCH, CHAN, TOKENS), jnp.float32),
            in_specs=[anywhere] * 6,
            out_specs=pl.BlockSpec(memory_space=pltpu.VMEM),
            scratch_shapes=[
                pltpu.VMEM((CHAN, DEV_TOK), jnp.float32),
                pltpu.VMEM((2, CHAN, HALF), jnp.bfloat16),
                pltpu.VMEM((2, CHAN, HALF), jnp.bfloat16),
                pltpu.VMEM((NM, NT, 2, 2, HALF), jnp.bfloat16),
                pltpu.VMEM((NT, 1, 2), jnp.float32),
                pltpu.VMEM((CHAN, HIDDEN), jnp.bfloat16),
                pltpu.VMEM((CHAN, HIDDEN), jnp.bfloat16),
                pltpu.VMEM((NT, 2, HIDDEN), jnp.float32),
                pltpu.VMEM((NT, 2, HIDDEN), jnp.float32),
                pltpu.VMEM((2, 2, CHAN, DEV_TOK), jnp.float32),
                pltpu.VMEM((CHUNKS, STEPS, CHAN, TM), jnp.float32),
                pltpu.SemaphoreType.DMA((7,)),
                pltpu.SemaphoreType.DMA((NM, NT)),
                pltpu.SemaphoreType.DMA((NM, NT)),
                pltpu.SemaphoreType.DMA((NT,)),
                pltpu.SemaphoreType.DMA((NT,)),
                pltpu.SemaphoreType.DMA,
                pltpu.SemaphoreType.DMA,
                pltpu.SemaphoreType.DMA((STEPS, CHUNKS, 2)),
                pltpu.SemaphoreType.DMA((NM, NT, 2, CHUNKS)),
            ],
            compiler_params=pltpu.CompilerParams(collective_id=0, has_side_effects=True),
        )(x_t, w_up, w_down.T, mod_scale, mod_shift, step_size.reshape(1, 2))
        return jnp.swapaxes(out, 2, 3)

    return jax.shard_map(device_body, mesh=mesh, in_specs=(P('data', None, None), P(None, 'model'), P('model', None), P('time', 'model'), P('time', 'model'), P('time')), out_specs=P('time', 'data', None, None), check_vma=False)
```

time: 38.6 us -> 29.6 us (0.77); the launches traced: 38.1 us -> 29.5 us
  Pallas kernels: 36.2 us -> 28.7 us
  local copies, waits for them, and re-layouts: 1.89 us -> 0.8 us
    pallas_call x1, Pallas kernels: 36.2 us -> 28.7 us  [device_body(): pl.pallas_call(kernel, out_shape=pltpu.VMEM((2, BATCH, CHAN, TOKENS), jnp...]
    unnamed x1, local copies, waits for them, and re-layouts: 1.89 us -> 0.8 us
where the time goes in v2:
time: 29.6 us; the launch traced here: 29.5 us
  Pallas kernels  28.7 us (97%)
  local copies, waits for them, and re-layouts  0.8 us (3%)
    pallas_call x1, Pallas kernels, device_body(): pl.pallas_call(kernel, out_shape=pltpu.VMEM((2, BATCH, CHAN, TOKENS), jnp...  28.7 us
    unnamed x1, local copies, waits for them, and re-layouts  0.8 us

profile of v2, /device:TPU:3, one launch (start us, length us, event | category | flops | bytes accessed | tf_op | source)
XLA Modules:
  0.0 29.5 jit_solution(7240548029426779477)
XLA Ops:
  0.0 28.7 %shard_map.64 = f32[2,4,16,1024]{3,2,1,0:T(8,128)S(1)} custom-call(f32[4,16,1024]{2,1,0:T(8,128)} %bitcast.5, bf16[16,576]{1,0:T(8,128)(2,1)} %up_ref.1, bf16[16,576]{1,0:T(8,128)(2,1)} %bitcast.6, bf16[2,576]{1,0:T(2,128)(2,1)} %gam_ref.1, bf16[2,576]{1,0:T(2,128)(2,1)} %bet_ref.1, f32[1,2]{1,0:T(1,128)} %bitcast.7), custom_call_target="tpu_custom_call" | custom-call | tf_op jit(solution)/shard_map/pallas_call | solution.py:263
  28.7 0.8 %copy.8 = f32[2,4,1024,16]{2,3,1,0:T(8,128)} copy(f32[2,4,1024,16]{2,3,1,0:T(8,128)S(1)} %bitcast.4) | data formatting | bytes 1048576

commit v3 on v2

--- a/solution.py
+++ b/solution.py
@@ -16,7 +16,8 @@
 DEV_TOK = BATCH * TOKENS // (NM * NT)
 CHUNKS = 2
 TM = DEV_TOK // CHUNKS
-HID_TILE = 1152
+HID_TILE = 256
+LOOK, LAG = 2, 1
 TANH_LIN = 0.7978845608028654
 TANH_CUB = TANH_LIN * 0.044715
 
@@ -26,20 +27,42 @@
     return half * jnp.tanh(inner) + half
 
 
-def drift(x_rows, scale_row, shift_row, w_up, w_down_t, lo, hi, tile=HID_TILE):
-    total = None
-    for at in range(lo, hi, tile):
-        cols = slice(at, min(at + tile, hi))
-        pre = jnp.dot(x_rows, w_up[:, cols], preferred_element_type=jnp.float32)
-        hidden = gelu_from_half(pre * scale_row[:, cols] + shift_row[:, cols])
-        part = lax.dot_general(w_down_t[:, cols], hidden.astype(jnp.bfloat16), (((1,), (1,)), ((), ())),
+def emit(units, w_up, w_down_t):
+    blocks = [(u, at, min(at + HID_TILE, u[3][1])) for u in units for at in range(u[3][0], u[3][1], HID_TILE)]
+    rows, pre, hidden, totals = {}, {}, {}, {}
+
+    def up(n):
+        unit, lo, hi = blocks[n]
+        if lo == unit[3][0]:
+            rows[id(unit)] = unit[0]().T.astype(jnp.bfloat16)
+        pre[n] = jnp.dot(rows[id(unit)], w_up[:, lo:hi], preferred_element_type=jnp.float32)
+
+    def act(n):
+        unit, lo, hi = blocks[n]
+        hidden[n] = gelu_from_half(pre.pop(n) * unit[1](lo, hi) + unit[2](lo, hi)).astype(jnp.bfloat16)
+
+    def down(n):
+        unit, lo, hi = blocks[n]
+        part = lax.dot_general(w_down_t[:, lo:hi], hidden.pop(n), (((1,), (1,)), ((), ())),
                                preferred_element_type=jnp.float32)
-        total = part if total is None else total + part
-    return total
+        totals[id(unit)] = part if lo == unit[3][0] else totals[id(unit)] + part
+        if hi == unit[3][1]:
+            unit[4](totals.pop(id(unit)))
+
+    for n in range(min(LOOK, len(blocks))):
+        up(n)
+    for n in range(len(blocks)):
+        if n + LOOK < len(blocks):
+            up(n + LOOK)
+        act(n)
+        if n >= LAG:
+            down(n - LAG)
+    for n in range(max(0, len(blocks) - LAG), len(blocks)):
+        down(n)
 
 
 def kernel(x_ref, up_ref, down_ref, gam_ref, bet_ref, step_ref, out_ref,
-           x0, w_own, w_other, rows, steps, w_up, w_down_t, scale, shift, first, final,
+           x0, w_own, w_other, rows, steps, w_up, w_down_t, scale, shift, first, final, tally,
            loc_sem, rsend, rrecv, hsend, hrecv, wsend, wrecv, osend, orecv):
     me_m = lax.axis_index("model")
     me_t = lax.axis_index("time")
@@ -78,11 +101,15 @@
 
     def first_pair(t):
         table(0, t, own_cols, own_cols)
-        for r in range(2):
-            for c in range(CHUNKS):
-                tok = slice(c * TM, (c + 1) * TM)
-                first[t, r, :, tok] = drift(x0[:, tok].T.astype(jnp.bfloat16), scale[t, r:r + 1, :], shift[t, r:r + 1, :],
-                                            w_up, w_down_t, 0, BODY)
+
+        def unit(r, c):
+            tok = slice(c * TM, (c + 1) * TM)
+
+            def done(total):
+                first[t, r, :, tok] = total
+            return (lambda: x0[:, tok], lambda lo, hi: scale[t, r:r + 1, lo:hi], lambda lo, hi: shift[t, r:r + 1, lo:hi],
+                    (0, BODY), done)
+        emit([unit(r, c) for r in range(2) for c in range(CHUNKS)], w_up, w_down_t)
 
     w_up[:, own_cols] = w_own[0][:, own_cols]
     w_down_t[:, own_cols] = w_own[1][:, own_cols]
@@ -129,8 +156,14 @@
         first_pair(1)
 
     arrived(w_other, wrecv)
-    rows_arrived(1, 0)
-    rows_arrived(1, 1)
+    for t in range(NT):
+        if t > 1:
+            rows_arrived(0, t)
+        rows_arrived(1, t)
+
+        @pl.when(me_t != t)
+        def _():
+            arrived(steps.at[t], hrecv.at[t])
 
     other_cols = slice(BODY, 2 * BODY)
     rest = slice(BODY, HALF)
@@ -148,17 +181,13 @@
         scale[t, :, rest_cols] = 0.5 * (1.0 + join(rows[0, t, 0].astype(jnp.float32), rows[1, t, 0].astype(jnp.float32)))
         shift[t, :, rest_cols] = 0.5 * join(rows[0, t, 1].astype(jnp.float32), rows[1, t, 1].astype(jnp.float32))
 
-    for t in range(2):
+    for t in range(NT):
+        if t > 1:
+            table(0, t, own_cols, own_cols)
         finish_table(t)
-
-    def evaluate(latent, j, lo):
-        return drift(latent.T.astype(jnp.bfloat16), scale[j // 2, j % 2:j % 2 + 1, :], shift[j // 2, j % 2:j % 2 + 1, :],
-                     w_up, w_down_t, lo, HIDDEN)
 
     def step_value(j):
         return steps[j // 2, :, j % 2:j % 2 + 1]
-
-    out_copies = []
 
     def place(j, c):
         return out_ref.at[j % 2, sample, :, pl.ds(pl.multiple_of(tok0 + c * TM, TM), TM)]
@@ -167,61 +196,42 @@
         owner = j // 2
         src = final.at[c, j]
         src[...] = value
-        dt = (owner + NT - me_t) % NT
-        far = pltpu.make_async_remote_copy(src, place(j, c), osend.at[j, c, 0], orecv.at[1, dt, j % 2, c],
+        far = pltpu.make_async_remote_copy(src, place(j, c), osend.at[0], orecv.at[j % 2],
                                            device_id=(0, (me_m + 1) % NM, owner), device_id_type=MESH)
         far.start()
-        near = pltpu.make_async_remote_copy(src, place(j, c), osend.at[j, c, 1], orecv.at[0, dt, j % 2, c],
+        near = pltpu.make_async_remote_copy(src, place(j, c), osend.at[1 + owner], orecv.at[j % 2],
                                             device_id=(0, me_m, owner), device_id_type=MESH)
-        out_copies.append((owner, far, near))
 
         @pl.when(me_t != owner)
         def _():
             near.start()
 
-    starts = [x0[:, c * TM:(c + 1) * TM] for c in range(CHUNKS)]
-    settled = [None] * CHUNKS
-    running = [None] * CHUNKS
-
-    def sweep_step(sweep, j, c, value):
-        value = step_value(j) * value
-        if j == sweep - 1:
-            running[c] = settled[c]
-        running[c] = value if running[c] is None else running[c] + value
-        fresh[c][j + 1] = starts[c] + running[c]
-        if j == sweep - 1:
-            settled[c] = running[c]
-        if j == sweep - 1 or sweep == SWEEPS:
-            publish(j + 1, c, fresh[c][j + 1])
-
-    for t in range(2):
-        @pl.when(me_t != t)
-        def _():
-            arrived(steps.at[t], hrecv.at[t])
-    fresh = [{} for _ in range(CHUNKS)]
-    for j in range(SWEEPS):
-        for c in range(CHUNKS):
-            value = first[j // 2, j % 2, :, c * TM:(c + 1) * TM] + evaluate(starts[c], j, BODY)
-            sweep_step(1, j, c, value)
-
-    for t in range(2, NT):
-        rows_arrived(0, t)
-        rows_arrived(1, t)
-
-        @pl.when(me_t != t)
-        def _():
-            arrived(steps.at[t], hrecv.at[t])
-
-        table(0, t, own_cols, own_cols)
-        finish_table(t)
-
-    latents = [None] * CHUNKS
-    for c, n in ORDER:
-        sweep, j = n // 4 + 1, n // 4 + n % 4
-        if n % 4 == 0:
-            latents[c] = fresh[c]
-            fresh[c] = {}
-        sweep_step(sweep, j, c, evaluate(latents[c][j], j, 0))
+    latents = {}
+    settled, running = {}, {}
+
+    def unit(sweep, j, c):
+        tok = slice(c * TM, (c + 1) * TM)
+
+        def latent():
+            return x0[:, tok] if sweep == 1 else latents[sweep - 1, j, c]
+
+        def done(total):
+            if sweep == 1:
+                total = first[j // 2, j % 2, :, tok] + total
+            value = step_value(j) * total
+            base = running[c] if j > sweep - 1 else settled.get(c)
+            running[c] = value if base is None else base + value
+            latents[sweep, j + 1, c] = x0[:, tok] + running[c]
+            if j == sweep - 1:
+                settled[c] = running[c]
+            if j == sweep - 1 or sweep == SWEEPS:
+                publish(j + 1, c, latents[sweep, j + 1, c])
+        row = slice(j % 2, j % 2 + 1)
+        return (latent, lambda lo, hi: scale[j // 2, row, lo:hi], lambda lo, hi: shift[j // 2, row, lo:hi],
+                (BODY if sweep == 1 else 0, HIDDEN), done)
+
+    emit([unit(sweep, j, c) for c in range(CHUNKS) for sweep in range(1, SWEEPS + 1) for j in range(sweep - 1, sweep + 3)],
+         w_up, w_down_t)
 
     for j in range(1, STEPS):
         @pl.when(me_t == j // 2)
@@ -231,29 +241,24 @@
 
     for copy in sends:
         copy.wait_send()
-    for owner, far, near in out_copies:
-        far.wait_send()
-
+    def drained(sem, count):
+        pltpu.make_async_copy(tally.at[pl.ds(0, count)], tally.at[pl.ds(0, count)], sem).wait()
+
+    drained(osend.at[0], CHUNKS * (STEPS - 1))
+    for owner in range(NT):
         @pl.when(me_t != owner)
         def _():
-            near.wait_send()
+            drained(osend.at[1 + owner], CHUNKS * (2 if owner else 1))
 
     @pl.when(me_t == 0)
     def _():
         keep.wait()
 
-    for r in range(2):
-        def arrivals():
-            for dm, dt in others:
-                for c in range(CHUNKS):
-                    arrived(place(r, c), orecv.at[dm, dt, r, c])
-        if r == 0:
-            pl.when(me_t > 0)(arrivals)
-        else:
-            arrivals()
-
-
-ORDER = [(c, n) for c in range(CHUNKS) for n in range(4, 16)]
+    @pl.when(me_t > 0)
+    def _():
+        drained(orecv.at[0], CHUNKS * len(others))
+
+    drained(orecv.at[1], CHUNKS * len(others))
 
 
 def solution(mesh):
@@ -277,6 +282,7 @@
                 pltpu.VMEM((NT, 2, HIDDEN), jnp.float32),
                 pltpu.VMEM((2, 2, CHAN, DEV_TOK), jnp.float32),
                 pltpu.VMEM((CHUNKS, STEPS, CHAN, TM), jnp.float32),
+                pltpu.VMEM((CHUNKS * (STEPS - 1), CHAN, TM), jnp.float32),
                 pltpu.SemaphoreType.DMA((7,)),
                 pltpu.SemaphoreType.DMA((NM, NT)),
                 pltpu.SemaphoreType.DMA((NM, NT)),
@@ -284,8 +290,8 @@
                 pltpu.SemaphoreType.DMA((NT,)),
                 pltpu.SemaphoreType.DMA,
                 pltpu.SemaphoreType.DMA,
-                pltpu.SemaphoreType.DMA((STEPS, CHUNKS, 2)),
-                pltpu.SemaphoreType.DMA((NM, NT, 2, CHUNKS)),
+                pltpu.SemaphoreType.DMA((1 + NT,)),
+                pltpu.SemaphoreType.DMA((2,)),
             ],
             compiler_params=pltpu.CompilerParams(collective_id=0, has_side_effects=True),
         )(x_t, w_up, w_down.T, mod_scale, mod_shift, step_size.reshape(1, 2))

time: 29.6 us -> 25.6 us (0.86)
  Pallas kernels: 28.7 us -> 24.7 us
    pallas_call x1, Pallas kernels: 28.7 us -> 24.7 us  [device_body(): pl.pallas_call(kernel, out_shape=pltpu.VMEM((2, BATCH, CHAN, TOKENS), jnp...]
where the time goes in v3:
time: 25.6 us; the launch traced here: 25.5 us
  Pallas kernels  24.7 us (96%)
  local copies, waits for them, and re-layouts  0.8 us (3%)
    pallas_call x1, Pallas kernels, device_body(): pl.pallas_call(kernel, out_shape=pltpu.VMEM((2, BATCH, CHAN, TOKENS), jnp...  24.7 us
    unnamed x1, local copies, waits for them, and re-layouts  0.8 us

profile of v3, /device:TPU:3, one launch (start us, length us, event | category | flops | bytes accessed | tf_op | source)
XLA Modules:
  0.0 25.5 jit_solution(13668690082309214460)
XLA Ops:
  0.0 24.7 %shard_map.64 = f32[2,4,16,1024]{3,2,1,0:T(8,128)S(1)} custom-call(f32[4,16,1024]{2,1,0:T(8,128)} %bitcast.5, bf16[16,576]{1,0:T(8,128)(2,1)} %up_ref.1, bf16[16,576]{1,0:T(8,128)(2,1)} %bitcast.6, bf16[2,576]{1,0:T(2,128)(2,1)} %gam_ref.1, bf16[2,576]{1,0:T(2,128)(2,1)} %bet_ref.1, f32[1,2]{1,0:T(1,128)} %bitcast.7), custom_call_target="tpu_custom_call" | custom-call | tf_op jit(solution)/shard_map/pallas_call | solution.py:268
  24.7 0.8 %copy.8 = f32[2,4,1024,16]{2,3,1,0:T(8,128)} copy(f32[2,4,1024,16]{2,3,1,0:T(8,128)S(1)} %bitcast.4) | data formatting | bytes 1048576

commit v4 on v3

--- a/solution.py
+++ b/solution.py
@@ -17,7 +17,8 @@
 CHUNKS = 2
 TM = DEV_TOK // CHUNKS
 HID_TILE = 256
-LOOK, LAG = 2, 1
+LOOK, LAG = 1, 1
+SEND_AFTER = {1: 1, 3: 2, 5: 4, 7: 6}
 TANH_LIN = 0.7978845608028654
 TANH_CUB = TANH_LIN * 0.044715
 
@@ -192,19 +193,17 @@
     def place(j, c):
         return out_ref.at[j % 2, sample, :, pl.ds(pl.multiple_of(tok0 + c * TM, TM), TM)]
 
-    def publish(j, c, value):
-        owner = j // 2
-        src = final.at[c, j]
-        src[...] = value
-        far = pltpu.make_async_remote_copy(src, place(j, c), osend.at[0], orecv.at[j % 2],
-                                           device_id=(0, (me_m + 1) % NM, owner), device_id_type=MESH)
-        far.start()
-        near = pltpu.make_async_remote_copy(src, place(j, c), osend.at[1 + owner], orecv.at[j % 2],
-                                            device_id=(0, me_m, owner), device_id_type=MESH)
+    def send_latents(first_j, last_j, c):
+        owner, count = first_j // 2, last_j - first_j + 1
+        src = final.at[c, pl.ds(first_j, count)]
+        dst = out_ref.at[pl.ds(first_j % 2, count), sample, :, pl.ds(pl.multiple_of(tok0 + c * TM, TM), TM)]
+        pltpu.make_async_remote_copy(src, dst, osend.at[0], orecv.at[0],
+                                     device_id=(0, (me_m + 1) % NM, owner), device_id_type=MESH).start()
 
         @pl.when(me_t != owner)
         def _():
-            near.start()
+            pltpu.make_async_remote_copy(src, dst, osend.at[1 + owner], orecv.at[0],
+                                         device_id=(0, me_m, owner), device_id_type=MESH).start()
 
     latents = {}
     settled, running = {}, {}
@@ -225,7 +224,9 @@
             if j == sweep - 1:
                 settled[c] = running[c]
             if j == sweep - 1 or sweep == SWEEPS:
-                publish(j + 1, c, latents[sweep, j + 1, c])
+                final[c, j + 1] = latents[sweep, j + 1, c]
+                if j + 1 in SEND_AFTER:
+                    send_latents(SEND_AFTER[j + 1], j + 1, c)
         row = slice(j % 2, j % 2 + 1)
         return (latent, lambda lo, hi: scale[j // 2, row, lo:hi], lambda lo, hi: shift[j // 2, row, lo:hi],
                 (BODY if sweep == 1 else 0, HIDDEN), done)
@@ -256,9 +257,11 @@
 
     @pl.when(me_t > 0)
     def _():
+        drained(orecv.at[0], 2 * CHUNKS * len(others))
+
+    @pl.when(me_t == 0)
+    def _():
         drained(orecv.at[0], CHUNKS * len(others))
-
-    drained(orecv.at[1], CHUNKS * len(others))
 
 
 def solution(mesh):
@@ -282,7 +285,7 @@
                 pltpu.VMEM((NT, 2, HIDDEN), jnp.float32),
                 pltpu.VMEM((2, 2, CHAN, DEV_TOK), jnp.float32),
                 pltpu.VMEM((CHUNKS, STEPS, CHAN, TM), jnp.float32),
-                pltpu.VMEM((CHUNKS * (STEPS - 1), CHAN, TM), jnp.float32),
+                pltpu.VMEM((2 * CHUNKS * (NM * NT - 1), CHAN, TM), jnp.float32),
                 pltpu.SemaphoreType.DMA((7,)),
                 pltpu.SemaphoreType.DMA((NM, NT)),
                 pltpu.SemaphoreType.DMA((NM, NT)),
@@ -291,7 +294,7 @@
                 pltpu.SemaphoreType.DMA,
                 pltpu.SemaphoreType.DMA,
                 pltpu.SemaphoreType.DMA((1 + NT,)),
-                pltpu.SemaphoreType.DMA((2,)),
+                pltpu.SemaphoreType.DMA((1,)),
             ],
             compiler_params=pltpu.CompilerParams(collective_id=0, has_side_effects=True),
         )(x_t, w_up, w_down.T, mod_scale, mod_shift, step_size.reshape(1, 2))

time: 25.6 us -> 24.6 us (0.961)
  Pallas kernels: 24.7 us -> 23.6 us
    pallas_call x1, Pallas kernels: 24.7 us -> 23.6 us  [device_body(): pl.pallas_call(kernel, out_shape=pltpu.VMEM((2, BATCH, CHAN, TOKENS), jnp...]
where the time goes in v4:
time: 24.6 us; the launch traced here: 24.4 us
  Pallas kernels  23.6 us (96%)
  local copies, waits for them, and re-layouts  0.8 us (3%)
    pallas_call x1, Pallas kernels, device_body(): pl.pallas_call(kernel, out_shape=pltpu.VMEM((2, BATCH, CHAN, TOKENS), jnp...  23.6 us
    unnamed x1, local copies, waits for them, and re-layouts  0.8 us

profile of v4, /device:TPU:3, one launch (start us, length us, event | category | flops | bytes accessed | tf_op | source)
XLA Modules:
  0.0 24.4 jit_solution(18382199352989361257)
XLA Ops:
  0.0 23.6 %shard_map.64 = f32[2,4,16,1024]{3,2,1,0:T(8,128)S(1)} custom-call(f32[4,16,1024]{2,1,0:T(8,128)} %bitcast.5, bf16[16,576]{1,0:T(8,128)(2,1)} %up_ref.1, bf16[16,576]{1,0:T(8,128)(2,1)} %bitcast.6, bf16[2,576]{1,0:T(2,128)(2,1)} %gam_ref.1, bf16[2,576]{1,0:T(2,128)(2,1)} %bet_ref.1, f32[1,2]{1,0:T(1,128)} %bitcast.7), custom_call_target="tpu_custom_call" | custom-call | tf_op jit(solution)/shard_map/pallas_call | solution.py:271
  23.6 0.8 %copy.8 = f32[2,4,1024,16]{2,3,1,0:T(8,128)} copy(f32[2,4,1024,16]{2,3,1,0:T(8,128)S(1)} %bitcast.4) | data formatting | bytes 1048576
